TPU v7x, 32 devices: a whole 2x2x4 slice. The times are simulated.
32 devices in a mesh: dp: 4 (over x, y), tp: 8 (over z, core).
Axes of the slice: x: 2, y: 2, z: 4, core: 2. Of those that a mesh axis runs over, the one named last changes fastest.
Arguments:
- x: bfloat16 [8192, 3072], P('dp'), parts along dimension 0
- w_gate: bfloat16 [3072, 8192], P(None, 'tp')
- w_up: bfloat16 [3072, 8192], P(None, 'tp')
- w_down: bfloat16 [8192, 3072], P('tp')
Outputs:
- output: bfloat16 [8192, 3072], P('dp'), parts along dimension 0
There are 4 independent parts. A program takes and returns all parts, laid end to end along the dimension named above; an argument that names none is the same for every part.
All inputs are finite; a program needn't handle non-finite values.
Results may differ from a plain program's by a relative error of at most 0.016.
Values are sent between devices in bfloat16 or wider.
A program may use at most 2 GiB of HBM per device.

v0:
```python
import jax
import jax.numpy as jnp
from jax import lax
from jax.sharding import PartitionSpec as P


def solution(mesh):
    def step(x, w_gate, w_up, w_down):
        gate = jnp.dot(x, w_gate, preferred_element_type=jnp.float32)
        up = jnp.dot(x, w_up, preferred_element_type=jnp.float32)
        hidden = (jax.nn.silu(gate) * up).astype(jnp.bfloat16)
        term = jnp.dot(hidden, w_down, preferred_element_type=jnp.float32).astype(jnp.bfloat16)
        return lax.psum(term, "tp")

    return jax.shard_map(
        step,
        mesh=mesh,
        in_specs=(P("dp", None), P(None, "tp"), P(None, "tp"), P("tp", None)),
        out_specs=P("dp", None),
        check_vma=False,
    )
```

profile of v0, /device:TPU:0, one launch (start us, length us, event | category | flops | bytes accessed | tf_op | source)
XLA Modules:
  0.0 337.8 jit_solution(14865776142590113137)
XLA Ops:
  6.5 0.0 all-reduce.2.cloned.1.call-start
  6.5 0.0 copy-start
  6.5 19.3 %fusion = f32[2048,1024]{1,0:T(8,128)} fusion(bf16[2048,3072]{1,0:T(8,128)(2,1)} %param.4, bf16[3072,1024]{1,0:T(8,128)(2,1)} %param.5), kind=kOutput, calls=%fused_computation.2 | convolution fusion | flops 12884901888 | bytes 27262976 | tf_op jit(solution)/shard_map/dot_general | solution.py:9
  25.9 0.0 copy-done
  25.9 18.8 %multiply_convert_fusion = bf16[2048,1024]{1,0:T(8,128)(2,1)S(1)} fusion(f32[2048,1024]{1,0:T(8,128)} %fusion, bf16[2048,3072]{1,0:T(8,128)(2,1)S(1)} %copy-done, bf16[3072,1024]{1,0:T(8,128)(2,1)} %param.6), kind=kOutput, calls=%fused_computation.1 | convolution fusion | flops 12897484800 | bytes 31457280 | tf_op jit(solution)/shard_map/dot_general | solution.py:10
  44.7 18.4 %convolution_convert_fusion = bf16[2048,3072]{1,0:T(8,128)(2,1)} fusion(bf16[2048,1024]{1,0:T(8,128)(2,1)S(1)} %multiply_convert_fusion, bf16[1024,3072]{1,0:T(8,128)(2,1)} %param.7), kind=kOutput, calls=%fused_computation | convolution fusion | flops 12891193344 | bytes 23068672 | tf_op jit(solution)/shard_map/dot_general | solution.py:12
  63.1 0.0 all-reduce.2.cloned.1.call-update
  63.1 257.3 %all-reduce.2.cloned.1.call-done = bf16[2048,3072]{1,0:T(8,128)(2,1)} async-done(((bf16[2048,3072]{1,0:T(8,128)(2,1)}), bf16[2048,3072]{1,0:T(8,128)(2,1)}) %all-reduce.2.cloned.1.call-update) | async-done | bytes 12582928 | tf_op jit(solution)/shard_map/psum | solution.py:13
  320.4 10.5 %copy.6 = bf16[2048,3072]{1,0:T(8,128)(2,1)} copy(bf16[2048,3072]{1,0:T(8,128)(2,1)} %all-reduce.2.cloned.1.call-done) | data formatting | bytes 25165824
Async XLA Ops:
  6.5 313.9 %all-reduce.2.cloned.1.call-start = ((), (), s32[]{:S(2)}) async-start(), calls=%async_computation | async-start | bytes 25165824 | tf_op jit(solution)/shard_map/psum | solution.py:13
  6.5 19.3 %copy-start = (bf16[2048,3072]{1,0:T(8,128)(2,1)S(1)}, bf16[2048,3072]{1,0:T(8,128)(2,1)}, u32[]{:S(2)}) copy-start(bf16[2048,3072]{1,0:T(8,128)(2,1)} %param.4) | copy-start | bytes 37748740
Sparse Core Ops, SparseCore 0:
  63.2 257.0 all-reduce.1
where the time goes:
time: 338 us
  waiting for transfers between devices  257 us (76%)
  matrix products  56.6 us (17%)
  between operations  13.4 us (4%)
  local copies, waits for them, and re-layouts  10.5 us (3%)
    psum x1, waiting for transfers between devices, step(): return lax.psum(term, 'tp')  257 us
    dot_general x1, matrix products, step(): gate = jnp.dot(x, w_gate, preferred_element_type=jnp.float32)  19.3 us
    dot_general x1, matrix products, step(): up = jnp.dot(x, w_up, preferred_element_type=jnp.float32)  18.8 us
    dot_general x1, matrix products, step(): jnp.dot(hidden, w_down, preferred_element_type=jnp.float32)  18.4 us
    unnamed x3, local copies, waits for them, and re-layouts  10.5 us
  transfers between devices with their start and end apart: 1, of which 1 were waited for; matrix products, arithmetic and copies ran while one was open for 0% of the time, Pallas kernels for 0%

commit v1 on v0

v1 whole, which is shorter than its diff:
```python
import functools

import jax
import jax.numpy as jnp
from jax import lax
from jax.experimental import pallas as pl
from jax.experimental.pallas import tpu as pltpu
from jax.sharding import PartitionSpec as P

MESH = pl.DeviceIdType.MESH
CHIPS = 4
CHUNK = 128
TILES = 4
RING = 8
STAGE = 4
SUM_LAG = (1, 3, 6, 3)
DONE_LAG = (12, 6, 12, 12)


def by_place(place, values):
    result = jnp.int32(values[-1])
    for k in range(len(values) - 1):
        result = jnp.where(place == k, jnp.int32(values[k]), result)
    return result


def kernel(
    chunk, tiles, x_hbm, gate_hbm, up_hbm, down_hbm, y_hbm,
    gate_w, up_w, down_w, x_buf, hidden, own, stage, theirs, low, high, sums,
    x_sem, gate_sem, up_sem, down_sem, stage_sem, theirs_sem, low_sem, high_sem,
    sum_sem, spread_sem, pass_sem, y_sem, give_sem, take_sem,
):
    rows, depth = x_hbm.shape
    units = gate_hbm.shape[1]
    half = rows // 2
    chunks = half // chunk
    pieces = chunks * tiles
    unit_tile = units // tiles
    col_tile = depth // tiles

    me = lax.axis_index("tp")
    chip, core = me // 2, me % 2
    place = jnp.where(core == 1, chip, CHIPS - 1 - chip)

    def at_place(k):
        return {"tp": jnp.where(core == 1, k, CHIPS - 1 - k) * 2 + core}

    other = {"tp": me + 1 - 2 * core}
    before, after = at_place(place - 1), at_place(place + 1)
    inner = jnp.logical_or(place == 1, place == 2)

    barrier = pltpu.get_barrier_semaphore()
    pl.semaphore_signal(barrier, inc=1, device_id=other, device_id_type=MESH)

    @pl.when(place > 0)
    def _():
        pl.semaphore_signal(barrier, inc=1, device_id=before, device_id_type=MESH)

    @pl.when(place < CHIPS - 1)
    def _():
        pl.semaphore_signal(barrier, inc=1, device_id=after, device_id_type=MESH)

    def x_rows(which, c):
        return x_hbm.at[pl.ds(pl.multiple_of(which * half + c * chunk, chunk), chunk), :]

    def fetch_x(c):
        slot = lax.rem(c, 2)
        pltpu.make_async_copy(x_rows(core, c), x_buf.at[slot, pl.ds(0, chunk)], x_sem.at[slot]).start()
        pltpu.make_async_copy(x_rows(1 - core, c), x_buf.at[slot, pl.ds(chunk, chunk)], x_sem.at[slot]).start()

    def wait_x(c):
        slot = lax.rem(c, 2)
        pltpu.make_async_copy(x_hbm.at[pl.ds(0, 2 * chunk), :], x_buf.at[slot], x_sem.at[slot]).wait()

    def unit_slice(t):
        return slice(t * unit_tile, (t + 1) * unit_tile)

    def col_slice(t):
        return slice(t * col_tile, (t + 1) * col_tile)

    def gate_copy(t):
        return pltpu.make_async_copy(gate_hbm.at[:, unit_slice(t)], gate_w.at[:, unit_slice(t)], gate_sem.at[t])

    def up_copy(t):
        return pltpu.make_async_copy(up_hbm.at[:, unit_slice(t)], up_w.at[:, unit_slice(t)], up_sem.at[t])

    def down_copy(t):
        return pltpu.make_async_copy(down_hbm.at[:, col_slice(t)], down_w.at[:, col_slice(t)], down_sem.at[t])

    fetch_x(0)
    for t in range(tiles):
        gate_copy(t).start()
        up_copy(t).start()
    fetch_x(1)
    for t in range(tiles):
        down_copy(t).start()

    def project(c, t):
        slot = lax.rem(c, 2)
        xs = x_buf[slot]
        gate = jnp.dot(xs, gate_w[:, unit_slice(t)], preferred_element_type=jnp.float32)
        up = jnp.dot(xs, up_w[:, unit_slice(t)], preferred_element_type=jnp.float32)
        hidden[slot, :, unit_slice(t)] = (jax.nn.silu(gate) * up).astype(jnp.bfloat16)

    def stage_copy(i):
        slot = lax.rem(i, STAGE)
        return pltpu.make_async_remote_copy(
            src_ref=stage.at[slot], dst_ref=theirs.at[i], send_sem=stage_sem.at[slot], recv_sem=theirs_sem.at[i],
            device_id=other, device_id_type=MESH,
        )

    def terms(c, t):
        i = c * tiles + t
        term = jnp.dot(hidden[lax.rem(c, 2)], down_w[:, col_slice(t)], preferred_element_type=jnp.float32)

        @pl.when(i >= STAGE)
        def _():
            stage_copy(i - STAGE).wait_send()

        stage[lax.rem(i, STAGE)] = term[chunk:].astype(jnp.bfloat16)
        stage_copy(i).start()
        own[lax.rem(i, RING)] = term[:chunk]

    def low_copy(p):
        return pltpu.make_async_remote_copy(
            src_ref=sums.at[p], dst_ref=low.at[p], send_sem=sum_sem, recv_sem=low_sem.at[p],
            device_id=after, device_id_type=MESH,
        )

    def high_copy(p):
        return pltpu.make_async_remote_copy(
            src_ref=sums.at[p], dst_ref=high.at[p], send_sem=sum_sem, recv_sem=high_sem.at[p],
            device_id=before, device_id_type=MESH,
        )

    def spread_copy(p):
        return pltpu.make_async_remote_copy(
            src_ref=sums.at[p], dst_ref=high.at[p], send_sem=spread_sem, recv_sem=high_sem.at[p],
            device_id=after, device_id_type=MESH,
        )

    def pass_copy(p):
        return pltpu.make_async_remote_copy(
            src_ref=high.at[p], dst_ref=high.at[p], send_sem=pass_sem, recv_sem=high_sem.at[p],
            device_id=before, device_id_type=MESH,
        )

    def deliver(src, p):
        c, t = p // tiles, lax.rem(p, tiles)
        block = y_hbm.at[
            pl.ds(pl.multiple_of(core * half + c * chunk, chunk), chunk),
            pl.ds(pl.multiple_of(t * col_tile, col_tile), col_tile),
        ]
        pltpu.make_async_remote_copy(
            src_ref=src, dst_ref=block, send_sem=give_sem, recv_sem=take_sem, device_id=other, device_id_type=MESH,
        ).start()
        pltpu.make_async_copy(src, block, y_sem).start()

    def combine(p):
        pltpu.make_async_copy(theirs.at[p], theirs.at[p], theirs_sem.at[p]).wait()

        def here():
            return own[lax.rem(p, RING)] + theirs[p].astype(jnp.float32)

        @pl.when(jnp.logical_not(inner))
        def _():
            sums[p] = here().astype(jnp.bfloat16)

        @pl.when(inner)
        def _():
            pltpu.make_async_copy(low.at[p], low.at[p], low_sem.at[p]).wait()

        @pl.when(place == 1)
        def _():
            sums[p] = (here() + low[p].astype(jnp.float32)).astype(jnp.bfloat16)

        @pl.when(place == 2)
        def _():
            pltpu.make_async_copy(high.at[p], high.at[p], high_sem.at[p]).wait()
            sums[p] = (here() + low[p].astype(jnp.float32) + high[p].astype(jnp.float32)).astype(jnp.bfloat16)

        @pl.when(place < 2)
        def _():
            low_copy(p).start()

        @pl.when(place >= 2)
        def _():
            high_copy(p).start()

        @pl.when(place == 2)
        def _():
            spread_copy(p).start()
            deliver(sums.at[p], p)

    def finish(p):
        pltpu.make_async_copy(high.at[p], high.at[p], high_sem.at[p]).wait()

        @pl.when(place == 1)
        def _():
            pass_copy(p).start()

        deliver(high.at[p], p)

    sum_lag = by_place(place, SUM_LAG)
    done_lag = by_place(place, DONE_LAG)

    def trail(i):
        p = i - sum_lag

        @pl.when(jnp.logical_and(p >= 0, p < pieces))
        def _():
            combine(p)

        d = i - done_lag

        @pl.when(jnp.logical_and(jnp.logical_and(d >= 0, d < pieces), place != 2))
        def _():
            finish(d)

    wait_x(0)
    for t in range(tiles):
        gate_copy(t).wait()
        up_copy(t).wait()
        project(0, t)
    for t in range(tiles):
        down_copy(t).wait()

    pl.semaphore_wait(barrier, jnp.where(inner, 3, 2))

    @pl.loop(0, chunks)
    def _(c):
        @pl.when(c + 2 < chunks)
        def _():
            fetch_x(c + 2)

        @pl.when(c + 1 < chunks)
        def _():
            wait_x(c + 1)

        for t in range(tiles):
            terms(c, t)

            @pl.when(c + 1 < chunks)
            def _():
                project(c + 1, t)

            trail(c * tiles + t)

    @pl.loop(pieces, pieces + max(SUM_LAG + DONE_LAG))
    def _(i):
        trail(i)

    for k in range(STAGE):
        stage_copy(pieces - STAGE + k).wait_send()
    pltpu.make_async_copy(sums, sums, sum_sem).wait()

    @pl.when(place == 2)
    def _():
        pltpu.make_async_copy(sums, sums, spread_sem).wait()

    @pl.when(place == 1)
    def _():
        pltpu.make_async_copy(high, high, pass_sem).wait()

    pltpu.make_async_copy(sums, sums, y_sem).wait()
    pltpu.make_async_copy(sums, sums, give_sem).wait()
    pltpu.make_async_copy(sums, sums, take_sem).wait()


def block(x, w_gate, w_up, w_down, chunk=CHUNK, tiles=TILES):
    rows, depth = x.shape
    units = w_gate.shape[1]
    pieces = rows // 2 // chunk * tiles
    piece = (chunk, depth // tiles)
    buffers = pltpu.VMEM((pieces,) + piece, jnp.bfloat16)
    dma = pltpu.SemaphoreType.DMA
    anywhere = pl.BlockSpec(memory_space=pl.ANY)
    return pl.pallas_call(
        functools.partial(kernel, chunk, tiles),
        out_shape=jax.ShapeDtypeStruct((rows, depth), jnp.bfloat16),
        in_specs=[anywhere] * 4,
        out_specs=anywhere,
        scratch_shapes=[
            pltpu.VMEM((depth, units), jnp.bfloat16),
            pltpu.VMEM((depth, units), jnp.bfloat16),
            pltpu.VMEM((units, depth), jnp.bfloat16),
            pltpu.VMEM((2, 2 * chunk, depth), jnp.bfloat16),
            pltpu.VMEM((2, 2 * chunk, units), jnp.bfloat16),
            pltpu.VMEM((RING,) + piece, jnp.float32),
            pltpu.VMEM((STAGE,) + piece, jnp.bfloat16),
            buffers, buffers, buffers, buffers,
            dma((2,)), dma((tiles,)), dma((tiles,)), dma((tiles,)), dma((STAGE,)),
            dma((pieces,)), dma((pieces,)), dma((pieces,)),
            dma, dma, dma, dma, dma, dma,
        ],
        compiler_params=pltpu.CompilerParams(
            collective_id=0, has_side_effects=True, vmem_limit_bytes=66_000_000
        ),
    )(x, w_gate, w_up, w_down)


def solution(mesh):
    return jax.shard_map(
        block,
        mesh=mesh,
        in_specs=(P("dp", None), P(None, "tp"), P(None, "tp"), P("tp", None)),
        out_specs=P("dp", None),
        check_vma=False,
    )
```

time: 338 us -> 177 us (0.52)
  waiting for transfers between devices: 257 us -> 0 us
  Pallas kernels: 0 us -> 166 us
  matrix products: 56.6 us -> 0 us
  between operations: 13.4 us -> 0.01 us
    psum x1 -> x0, waiting for transfers between devices: 257 us -> none  [step(): return lax.psum(term, 'tp')]
    pallas_call x0 -> x1, Pallas kernels: none -> 166 us  [block(): pl.pallas_call(functools.partial(kernel, chunk, tiles), out_shape=jax.Sha...]
    dot_general x3 -> x0, matrix products: 56.6 us -> none  [the longest x1 19.3 us: step(): gate = jnp.dot(x, w_gate, preferred_element_type=jnp.float32)]
    unnamed x3 -> x1, local copies, waits for them, and re-layouts: 10.5 us -> 10.5 us
  transfers between devices with their start and end apart: 1 -> 0, of which waited for: 1 -> 0; matrix products, arithmetic and copies ran while one was open for 0% -> 0% of each run, Pallas kernels for 0% -> 0%
where the time goes in v1:
time: 177 us
  Pallas kernels  166 us (94%)
  local copies, waits for them, and re-layouts  10.5 us (6%)
    pallas_call x1, Pallas kernels, block(): pl.pallas_call(functools.partial(kernel, chunk, tiles), out_shape=jax.Sha...  166 us
    unnamed x1, local copies, waits for them, and re-layouts  10.5 us

profile of v1, /device:TPU:0, one launch (start us, length us, event | category | flops | bytes accessed | tf_op | source)
XLA Modules:
  0.0 176.7 jit_solution(10353377749576469719)
XLA Ops:
  0.0 166.2 %shard_map.46 = bf16[2048,3072]{1,0:T(8,128)(2,1)} custom-call(bf16[2048,3072]{1,0:T(8,128)(2,1)} %x_hbm.1, bf16[3072,1024]{1,0:T(8,128)(2,1)} %gate_hbm.1, bf16[3072,1024]{1,0:T(8,128)(2,1)} %up_hbm.1, bf16[1024,3072]{1,0:T(8,128)(2,1)} %down_hbm.1), custom_call_target="tpu_custom_call" | custom-call | tf_op jit(solution)/shard_map/pallas_call | solution.py:278
  166.2 10.5 %copy.6 = bf16[2048,3072]{1,0:T(8,128)(2,1)} copy(bf16[2048,3072]{1,0:T(8,128)(2,1)} %shard_map.46) | data formatting | bytes 25165824

commit v2 on v1

--- a/solution.py
+++ b/solution.py
@@ -9,12 +9,12 @@
 
 MESH = pl.DeviceIdType.MESH
 CHIPS = 4
-CHUNK = 128
+CHUNK = 64
 TILES = 4
-RING = 8
+RING = 16
 STAGE = 4
-SUM_LAG = (1, 3, 6, 3)
-DONE_LAG = (12, 6, 12, 12)
+SUM_LAG = (1, 4, 10, 5)
+DONE_LAG = (24, 9, 24, 24)
 
 
 def by_place(place, values):

time: 177 us -> 172 us (0.972)
  Pallas kernels: 166 us -> 161 us
    pallas_call x1, Pallas kernels: 166 us -> 161 us  [block(): pl.pallas_call(functools.partial(kernel, chunk, tiles), out_shape=jax.Sha...]
where the time goes in v2:
time: 172 us
  Pallas kernels  161 us (94%)
  local copies, waits for them, and re-layouts  10.5 us (6%)
    pallas_call x1, Pallas kernels, block(): pl.pallas_call(functools.partial(kernel, chunk, tiles), out_shape=jax.Sha...  161 us
    unnamed x1, local copies, waits for them, and re-layouts  10.5 us

profile of v2, /device:TPU:0, one launch (start us, length us, event | category | flops | bytes accessed | tf_op | source)
XLA Modules:
  0.0 171.9 jit_solution(9586219453977419436)
XLA Ops:
  0.0 161.3 %shard_map.46 = bf16[2048,3072]{1,0:T(8,128)(2,1)} custom-call(bf16[2048,3072]{1,0:T(8,128)(2,1)} %x_hbm.1, bf16[3072,1024]{1,0:T(8,128)(2,1)} %gate_hbm.1, bf16[3072,1024]{1,0:T(8,128)(2,1)} %up_hbm.1, bf16[1024,3072]{1,0:T(8,128)(2,1)} %down_hbm.1), custom_call_target="tpu_custom_call" | custom-call | tf_op jit(solution)/shard_map/pallas_call | solution.py:278
  161.3 10.5 %copy.6 = bf16[2048,3072]{1,0:T(8,128)(2,1)} copy(bf16[2048,3072]{1,0:T(8,128)(2,1)} %shard_map.46) | data formatting | bytes 25165824

commit v3 on v2

--- a/solution.py
+++ b/solution.py
@@ -13,6 +13,8 @@
 TILES = 4
 RING = 16
 STAGE = 4
+OUT_COPIES = 16
+OUT_LIMIT = 1_000_000
 SUM_LAG = (1, 4, 10, 5)
 DONE_LAG = (24, 9, 24, 24)
 
@@ -267,6 +269,14 @@
     pltpu.make_async_copy(sums, sums, take_sem).wait()
 
 
+def put_out(y_vmem, y_hbm, sem):
+    rows = y_vmem.shape[0] // OUT_COPIES
+    for k in range(OUT_COPIES):
+        part = pl.ds(k * rows, rows)
+        pltpu.make_async_copy(y_vmem.at[part], y_hbm.at[part], sem).start()
+    pltpu.make_async_copy(y_vmem, y_hbm, sem).wait()
+
+
 def block(x, w_gate, w_up, w_down, chunk=CHUNK, tiles=TILES):
     rows, depth = x.shape
     units = w_gate.shape[1]
@@ -275,9 +285,9 @@
     buffers = pltpu.VMEM((pieces,) + piece, jnp.bfloat16)
     dma = pltpu.SemaphoreType.DMA
     anywhere = pl.BlockSpec(memory_space=pl.ANY)
-    return pl.pallas_call(
+    y = pl.pallas_call(
         functools.partial(kernel, chunk, tiles),
-        out_shape=jax.ShapeDtypeStruct((rows, depth), jnp.bfloat16),
+        out_shape=pltpu.VMEM((rows, depth), jnp.bfloat16),
         in_specs=[anywhere] * 4,
         out_specs=anywhere,
         scratch_shapes=[
@@ -294,9 +304,17 @@
             dma, dma, dma, dma, dma, dma,
         ],
         compiler_params=pltpu.CompilerParams(
-            collective_id=0, has_side_effects=True, vmem_limit_bytes=66_000_000
+            collective_id=0, has_side_effects=True, vmem_limit_bytes=54_000_000
         ),
     )(x, w_gate, w_up, w_down)
+    return pl.pallas_call(
+        put_out,
+        out_shape=jax.ShapeDtypeStruct((rows, depth), jnp.bfloat16),
+        in_specs=[anywhere],
+        out_specs=anywhere,
+        scratch_shapes=[dma],
+        compiler_params=pltpu.CompilerParams(vmem_limit_bytes=OUT_LIMIT),
+    )(y)
 
 
 def solution(mesh):

time: 172 us -> 166 us (0.965)
  local copies, waits for them, and re-layouts: 10.5 us -> 0 us
  Pallas kernels: 161 us -> 166 us
    unnamed x1 -> x0, local copies, waits for them, and re-layouts: 10.5 us -> none
    pallas_call x1 -> x2, Pallas kernels: 161 us -> 166 us  [the longest x1 161 us: block(): pl.pallas_call(functools.partial(kernel, chunk, tiles), out_shape=pltpu.V...]
where the time goes in v3:
time: 166 us
  Pallas kernels  166 us (100%)
    pallas_call x1, Pallas kernels, block(): pl.pallas_call(functools.partial(kernel, chunk, tiles), out_shape=pltpu.V...  161 us
    pallas_call x1, Pallas kernels, block(): pl.pallas_call(put_out, out_shape=jax.ShapeDtypeStruct((rows, depth), jnp...  4.57 us

profile of v3, /device:TPU:0, one launch (start us, length us, event | category | flops | bytes accessed | tf_op | source)
XLA Modules:
  0.0 165.7 jit_solution(4230153057787645946)
XLA Ops:
  0.0 161.2 %shard_map.46.y_vmem = bf16[2048,3072]{1,0:T(8,128)(2,1)S(1)} custom-call(bf16[2048,3072]{1,0:T(8,128)(2,1)} %x_hbm.1, bf16[3072,1024]{1,0:T(8,128)(2,1)} %gate_hbm.1, bf16[3072,1024]{1,0:T(8,128)(2,1)} %up_hbm.1, bf16[1024,3072]{1,0:T(8,128)(2,1)} %down_hbm.1), custom_call_target="tpu_custom_call" | custom-call | tf_op jit(solution)/shard_map/pallas_call | solution.py:288
  161.2 4.6 %shard_map.47 = bf16[2048,3072]{1,0:T(8,128)(2,1)} custom-call(bf16[2048,3072]{1,0:T(8,128)(2,1)S(1)} %shard_map.46.y_vmem), custom_call_target="tpu_custom_call" | custom-call | tf_op jit(solution)/shard_map/pallas_call | solution.py:310

commit v4 on v3

--- a/solution.py
+++ b/solution.py
@@ -15,8 +15,8 @@
 STAGE = 4
 OUT_COPIES = 16
 OUT_LIMIT = 1_000_000
-SUM_LAG = (1, 4, 10, 5)
-DONE_LAG = (24, 9, 24, 24)
+SUM_LAG = (0, 2, 5, 3)
+DONE_LAG = (24, 6, 24, 24)
 
 
 def by_place(place, values):
@@ -93,10 +93,6 @@
     for t in range(tiles):
         gate_copy(t).start()
         up_copy(t).start()
-    fetch_x(1)
-    for t in range(tiles):
-        down_copy(t).start()
-
     def project(c, t):
         slot = lax.rem(c, 2)
         xs = x_buf[slot]
@@ -223,6 +219,10 @@
     for t in range(tiles):
         gate_copy(t).wait()
         up_copy(t).wait()
+        if t == tiles // 2:
+            for k in range(tiles):
+                down_copy(k).start()
+            fetch_x(1)
         project(0, t)
     for t in range(tiles):
         down_copy(t).wait()

time: 166 us -> 165 us (level)
  no operation moved by 1% of the time
where the time goes in v4:
time: 165 us
  Pallas kernels  165 us (100%)
    pallas_call x1, Pallas kernels, block(): pl.pallas_call(functools.partial(kernel, chunk, tiles), out_shape=pltpu.V...  161 us
    pallas_call x1, Pallas kernels, block(): pl.pallas_call(put_out, out_shape=jax.ShapeDtypeStruct((rows, depth), jnp...  4.57 us

profile of v4, /device:TPU:0, one launch (start us, length us, event | category | flops | bytes accessed | tf_op | source)
XLA Modules:
  0.0 165.2 jit_solution(14682732459344949132)
XLA Ops:
  0.0 160.6 %shard_map.46.y_vmem = bf16[2048,3072]{1,0:T(8,128)(2,1)S(1)} custom-call(bf16[2048,3072]{1,0:T(8,128)(2,1)} %x_hbm.1, bf16[3072,1024]{1,0:T(8,128)(2,1)} %gate_hbm.1, bf16[3072,1024]{1,0:T(8,128)(2,1)} %up_hbm.1, bf16[1024,3072]{1,0:T(8,128)(2,1)} %down_hbm.1), custom_call_target="tpu_custom_call" | custom-call | tf_op jit(solution)/shard_map/pallas_call | solution.py:288
  160.6 4.6 %shard_map.47 = bf16[2048,3072]{1,0:T(8,128)(2,1)} custom-call(bf16[2048,3072]{1,0:T(8,128)(2,1)S(1)} %shard_map.46.y_vmem), custom_call_target="tpu_custom_call" | custom-call | tf_op jit(solution)/shard_map/pallas_call | solution.py:310

commit v5 on v4

--- a/solution.py
+++ b/solution.py
@@ -28,7 +28,7 @@
 
 def kernel(
     chunk, tiles, x_hbm, gate_hbm, up_hbm, down_hbm, y_hbm,
-    gate_w, up_w, down_w, x_buf, hidden, own, stage, theirs, low, high, sums,
+    gate_w, up_w, down_w, x_buf, hidden, first_gate, first_up, own, stage, theirs, low, high, sums,
     x_sem, gate_sem, up_sem, down_sem, stage_sem, theirs_sem, low_sem, high_sem,
     sum_sem, spread_sem, pass_sem, y_sem, give_sem, take_sem,
 ):
@@ -74,31 +74,41 @@
         slot = lax.rem(c, 2)
         pltpu.make_async_copy(x_hbm.at[pl.ds(0, 2 * chunk), :], x_buf.at[slot], x_sem.at[slot]).wait()
 
+    depth_tile = depth // tiles
+
     def unit_slice(t):
-        return slice(t * unit_tile, (t + 1) * unit_tile)
+        return pl.ds(pl.multiple_of(t * unit_tile, unit_tile), unit_tile)
+
+    def depth_slice(k):
+        return pl.ds(pl.multiple_of(k * depth_tile, depth_tile), depth_tile)
 
     def col_slice(t):
-        return slice(t * col_tile, (t + 1) * col_tile)
-
-    def gate_copy(t):
-        return pltpu.make_async_copy(gate_hbm.at[:, unit_slice(t)], gate_w.at[:, unit_slice(t)], gate_sem.at[t])
-
-    def up_copy(t):
-        return pltpu.make_async_copy(up_hbm.at[:, unit_slice(t)], up_w.at[:, unit_slice(t)], up_sem.at[t])
+        return pl.ds(pl.multiple_of(t * col_tile, col_tile), col_tile)
+
+    def gate_copy(k):
+        return pltpu.make_async_copy(gate_hbm.at[depth_slice(k)], gate_w.at[depth_slice(k)], gate_sem.at[k])
+
+    def up_copy(k):
+        return pltpu.make_async_copy(up_hbm.at[depth_slice(k)], up_w.at[depth_slice(k)], up_sem.at[k])
 
     def down_copy(t):
         return pltpu.make_async_copy(down_hbm.at[:, col_slice(t)], down_w.at[:, col_slice(t)], down_sem.at[t])
 
-    fetch_x(0)
-    for t in range(tiles):
-        gate_copy(t).start()
-        up_copy(t).start()
+    def dot(a, b):
+        return jnp.dot(a, b, preferred_element_type=jnp.float32)
+
+    def activate(gate, up):
+        return (jax.nn.silu(gate) * up).astype(jnp.bfloat16)
+
     def project(c, t):
         slot = lax.rem(c, 2)
         xs = x_buf[slot]
-        gate = jnp.dot(xs, gate_w[:, unit_slice(t)], preferred_element_type=jnp.float32)
-        up = jnp.dot(xs, up_w[:, unit_slice(t)], preferred_element_type=jnp.float32)
-        hidden[slot, :, unit_slice(t)] = (jax.nn.silu(gate) * up).astype(jnp.bfloat16)
+        hidden[slot, :, unit_slice(t)] = activate(dot(xs, gate_w[:, unit_slice(t)]), dot(xs, up_w[:, unit_slice(t)]))
+
+    fetch_x(0)
+    for k in range(tiles):
+        gate_copy(k).start()
+        up_copy(k).start()
 
     def stage_copy(i):
         slot = lax.rem(i, STAGE)
@@ -109,7 +119,7 @@
 
     def terms(c, t):
         i = c * tiles + t
-        term = jnp.dot(hidden[lax.rem(c, 2)], down_w[:, col_slice(t)], preferred_element_type=jnp.float32)
+        term = dot(hidden[lax.rem(c, 2)], down_w[:, col_slice(t)])
 
         @pl.when(i >= STAGE)
         def _():
@@ -216,40 +226,59 @@
             finish(d)
 
     wait_x(0)
-    for t in range(tiles):
-        gate_copy(t).wait()
-        up_copy(t).wait()
-        if t == tiles // 2:
-            for k in range(tiles):
-                down_copy(k).start()
+
+    @pl.loop(0, tiles)
+    def _(k):
+        gate_copy(k).wait()
+        up_copy(k).wait()
+
+        @pl.when(k == tiles // 2)
+        def _():
+            for t in range(tiles):
+                down_copy(t).start()
             fetch_x(1)
-        project(0, t)
-    for t in range(tiles):
-        down_copy(t).wait()
-
+
+        xs = x_buf[0, :, depth_slice(k)]
+        gate = dot(xs, gate_w[depth_slice(k)])
+        up = dot(xs, up_w[depth_slice(k)])
+
+        @pl.when(k == 0)
+        def _():
+            first_gate[...] = gate
+            first_up[...] = up
+
+        @pl.when(k > 0)
+        def _():
+            first_gate[...] += gate
+            first_up[...] += up
+
+    hidden[0] = activate(first_gate[...], first_up[...])
     pl.semaphore_wait(barrier, jnp.where(inner, 3, 2))
 
-    @pl.loop(0, chunks)
-    def _(c):
-        @pl.when(c + 2 < chunks)
-        def _():
-            fetch_x(c + 2)
-
-        @pl.when(c + 1 < chunks)
-        def _():
-            wait_x(c + 1)
-
-        for t in range(tiles):
+    @pl.loop(0, pieces + max(SUM_LAG + DONE_LAG))
+    def _(i):
+        c, t = i // tiles, lax.rem(i, tiles)
+
+        @pl.when(i < pieces)
+        def _():
+            @pl.when(c == 0)
+            def _():
+                down_copy(t).wait()
+
+            @pl.when(jnp.logical_and(t == 0, c + 2 < chunks))
+            def _():
+                fetch_x(c + 2)
+
+            @pl.when(jnp.logical_and(t == 0, c + 1 < chunks))
+            def _():
+                wait_x(c + 1)
+
             terms(c, t)
 
             @pl.when(c + 1 < chunks)
             def _():
                 project(c + 1, t)
 
-            trail(c * tiles + t)
-
-    @pl.loop(pieces, pieces + max(SUM_LAG + DONE_LAG))
-    def _(i):
         trail(i)
 
     for k in range(STAGE):
@@ -296,6 +325,8 @@
             pltpu.VMEM((units, depth), jnp.bfloat16),
             pltpu.VMEM((2, 2 * chunk, depth), jnp.bfloat16),
             pltpu.VMEM((2, 2 * chunk, units), jnp.bfloat16),
+            pltpu.VMEM((2 * chunk, units), jnp.float32),
+            pltpu.VMEM((2 * chunk, units), jnp.float32),
             pltpu.VMEM((RING,) + piece, jnp.float32),
             pltpu.VMEM((STAGE,) + piece, jnp.bfloat16),
             buffers, buffers, buffers, buffers,

time: 165 us -> 164 us (level)
  no operation moved by 1% of the time
where the time goes in v5:
time: 164 us
  Pallas kernels  164 us (100%)
    pallas_call x1, Pallas kernels, block(): pl.pallas_call(functools.partial(kernel, chunk, tiles), out_shape=pltpu.V...  160 us
    pallas_call x1, Pallas kernels, block(): pl.pallas_call(put_out, out_shape=jax.ShapeDtypeStruct((rows, depth), jnp...  4.57 us

profile of v5, /device:TPU:0, one launch (start us, length us, event | category | flops | bytes accessed | tf_op | source)
XLA Modules:
  0.0 164.2 jit_solution(7398883945936107860)
XLA Ops:
  0.0 159.7 %shard_map.46.y_vmem = bf16[2048,3072]{1,0:T(8,128)(2,1)S(1)} custom-call(bf16[2048,3072]{1,0:T(8,128)(2,1)} %x_hbm.1, bf16[3072,1024]{1,0:T(8,128)(2,1)} %gate_hbm.1, bf16[3072,1024]{1,0:T(8,128)(2,1)} %up_hbm.1, bf16[1024,3072]{1,0:T(8,128)(2,1)} %down_hbm.1), custom_call_target="tpu_custom_call" | custom-call | tf_op jit(solution)/shard_map/pallas_call | solution.py:317
  159.7 4.6 %shard_map.47 = bf16[2048,3072]{1,0:T(8,128)(2,1)} custom-call(bf16[2048,3072]{1,0:T(8,128)(2,1)S(1)} %shard_map.46.y_vmem), custom_call_target="tpu_custom_call" | custom-call | tf_op jit(solution)/shard_map/pallas_call | solution.py:341

commit v6 on v5

--- a/solution.py
+++ b/solution.py
@@ -15,15 +15,22 @@
 STAGE = 4
 OUT_COPIES = 16
 OUT_LIMIT = 1_000_000
-SUM_LAG = (0, 2, 5, 3)
-DONE_LAG = (24, 6, 24, 24)
-
-
-def by_place(place, values):
-    result = jnp.int32(values[-1])
-    for k in range(len(values) - 1):
-        result = jnp.where(place == k, jnp.int32(values[k]), result)
+SUM_LAG = ((0, 2, 4, 3), (0, 2, 4, 5))
+DONE_LAG = ((24, 7, 24, 24), (24, 6, 24, 24))
+PARTS = 2
+HEAD = 8
+AHEAD = 4
+
+
+def by_place(core, place, rows):
+    result = jnp.int32(rows[-1][-1])
+    for k, row in enumerate(rows):
+        for j, value in enumerate(row):
+            result = jnp.where(jnp.logical_and(core == k, place == j), jnp.int32(value), result)
     return result
+
+
+LONGEST = max(max(row) for row in SUM_LAG + DONE_LAG)
 
 
 def kernel(
@@ -74,7 +81,8 @@
         slot = lax.rem(c, 2)
         pltpu.make_async_copy(x_hbm.at[pl.ds(0, 2 * chunk), :], x_buf.at[slot], x_sem.at[slot]).wait()
 
-    depth_tile = depth // tiles
+    depth_tile = depth // HEAD
+    part_tile = col_tile // PARTS
 
     def unit_slice(t):
         return pl.ds(pl.multiple_of(t * unit_tile, unit_tile), unit_tile)
@@ -106,7 +114,7 @@
         hidden[slot, :, unit_slice(t)] = activate(dot(xs, gate_w[:, unit_slice(t)]), dot(xs, up_w[:, unit_slice(t)]))
 
     fetch_x(0)
-    for k in range(tiles):
+    for k in range(AHEAD):
         gate_copy(k).start()
         up_copy(k).start()
 
@@ -153,11 +161,12 @@
             device_id=before, device_id_type=MESH,
         )
 
-    def deliver(src, p):
-        c, t = p // tiles, lax.rem(p, tiles)
+    def deliver(src, m):
+        p = m // PARTS
+        c, column = p // tiles, lax.rem(p, tiles) * col_tile + lax.rem(m, PARTS) * part_tile
         block = y_hbm.at[
             pl.ds(pl.multiple_of(core * half + c * chunk, chunk), chunk),
-            pl.ds(pl.multiple_of(t * col_tile, col_tile), col_tile),
+            pl.ds(pl.multiple_of(column, part_tile), part_tile),
         ]
         pltpu.make_async_remote_copy(
             src_ref=src, dst_ref=block, send_sem=give_sem, recv_sem=take_sem, device_id=other, device_id_type=MESH,
@@ -166,51 +175,59 @@
 
     def combine(p):
         pltpu.make_async_copy(theirs.at[p], theirs.at[p], theirs_sem.at[p]).wait()
+        for part in range(PARTS):
+            combine_part(p, part)
+
+    def combine_part(p, part):
+        m = p * PARTS + part
+        columns = slice(part * part_tile, (part + 1) * part_tile)
 
         def here():
-            return own[lax.rem(p, RING)] + theirs[p].astype(jnp.float32)
+            return own[lax.rem(p, RING), :, columns] + theirs[p, :, columns].astype(jnp.float32)
 
         @pl.when(jnp.logical_not(inner))
         def _():
-            sums[p] = here().astype(jnp.bfloat16)
+            sums[m] = here().astype(jnp.bfloat16)
 
         @pl.when(inner)
         def _():
-            pltpu.make_async_copy(low.at[p], low.at[p], low_sem.at[p]).wait()
+            pltpu.make_async_copy(low.at[m], low.at[m], low_sem.at[m]).wait()
 
         @pl.when(place == 1)
         def _():
-            sums[p] = (here() + low[p].astype(jnp.float32)).astype(jnp.bfloat16)
+            sums[m] = (here() + low[m].astype(jnp.float32)).astype(jnp.bfloat16)
 
         @pl.when(place == 2)
         def _():
-            pltpu.make_async_copy(high.at[p], high.at[p], high_sem.at[p]).wait()
-            sums[p] = (here() + low[p].astype(jnp.float32) + high[p].astype(jnp.float32)).astype(jnp.bfloat16)
+            pltpu.make_async_copy(high.at[m], high.at[m], high_sem.at[m]).wait()
+            sums[m] = (here() + low[m].astype(jnp.float32) + high[m].astype(jnp.float32)).astype(jnp.bfloat16)
 
         @pl.when(place < 2)
         def _():
-            low_copy(p).start()
+            low_copy(m).start()
 
         @pl.when(place >= 2)
         def _():
-            high_copy(p).start()
+            high_copy(m).start()
 
         @pl.when(place == 2)
         def _():
-            spread_copy(p).start()
-            deliver(sums.at[p], p)
+            spread_copy(m).start()
+            deliver(sums.at[m], m)
 
     def finish(p):
-        pltpu.make_async_copy(high.at[p], high.at[p], high_sem.at[p]).wait()
-
-        @pl.when(place == 1)
-        def _():
-            pass_copy(p).start()
-
-        deliver(high.at[p], p)
-
-    sum_lag = by_place(place, SUM_LAG)
-    done_lag = by_place(place, DONE_LAG)
+        for part in range(PARTS):
+            m = p * PARTS + part
+            pltpu.make_async_copy(high.at[m], high.at[m], high_sem.at[m]).wait()
+
+            @pl.when(place == 1)
+            def _():
+                pass_copy(m).start()
+
+            deliver(high.at[m], m)
+
+    sum_lag = by_place(core, place, SUM_LAG)
+    done_lag = by_place(core, place, DONE_LAG)
 
     def trail(i):
         p = i - sum_lag
@@ -227,15 +244,22 @@
 
     wait_x(0)
 
-    @pl.loop(0, tiles)
+    @pl.loop(0, HEAD)
     def _(k):
         gate_copy(k).wait()
         up_copy(k).wait()
 
-        @pl.when(k == tiles // 2)
-        def _():
-            for t in range(tiles):
-                down_copy(t).start()
+        @pl.when(k + AHEAD < HEAD)
+        def _():
+            gate_copy(k + AHEAD).start()
+            up_copy(k + AHEAD).start()
+
+        @pl.when(k + AHEAD >= HEAD)
+        def _():
+            down_copy(k + AHEAD - HEAD).start()
+
+        @pl.when(k == HEAD - 1)
+        def _():
             fetch_x(1)
 
         xs = x_buf[0, :, depth_slice(k)]
@@ -255,7 +279,7 @@
     hidden[0] = activate(first_gate[...], first_up[...])
     pl.semaphore_wait(barrier, jnp.where(inner, 3, 2))
 
-    @pl.loop(0, pieces + max(SUM_LAG + DONE_LAG))
+    @pl.loop(0, pieces + LONGEST)
     def _(i):
         c, t = i // tiles, lax.rem(i, tiles)
 
@@ -311,7 +335,8 @@
     units = w_gate.shape[1]
     pieces = rows // 2 // chunk * tiles
     piece = (chunk, depth // tiles)
-    buffers = pltpu.VMEM((pieces,) + piece, jnp.bfloat16)
+    messages = pieces * PARTS
+    buffers = pltpu.VMEM((messages, chunk, depth // tiles // PARTS), jnp.bfloat16)
     dma = pltpu.SemaphoreType.DMA
     anywhere = pl.BlockSpec(memory_space=pl.ANY)
     y = pl.pallas_call(
@@ -329,9 +354,9 @@
             pltpu.VMEM((2 * chunk, units), jnp.float32),
             pltpu.VMEM((RING,) + piece, jnp.float32),
             pltpu.VMEM((STAGE,) + piece, jnp.bfloat16),
-            buffers, buffers, buffers, buffers,
-            dma((2,)), dma((tiles,)), dma((tiles,)), dma((tiles,)), dma((STAGE,)),
-            dma((pieces,)), dma((pieces,)), dma((pieces,)),
+            pltpu.VMEM((pieces,) + piece, jnp.bfloat16), buffers, buffers, buffers,
+            dma((2,)), dma((HEAD,)), dma((HEAD,)), dma((tiles,)), dma((STAGE,)),
+            dma((pieces,)), dma((messages,)), dma((messages,)),
             dma, dma, dma, dma, dma, dma,
         ],
         compiler_params=pltpu.CompilerParams(

time: 164 us -> 165 us (level)
  no operation moved by 1% of the time
where the time goes in v6:
time: 165 us
  Pallas kernels  165 us (100%)
    pallas_call x1, Pallas kernels, block(): pl.pallas_call(functools.partial(kernel, chunk, tiles), out_shape=pltpu.V...  161 us
    pallas_call x1, Pallas kernels, block(): pl.pallas_call(put_out, out_shape=jax.ShapeDtypeStruct((rows, depth), jnp...  4.57 us

profile of v6, /device:TPU:0, one launch (start us, length us, event | category | flops | bytes accessed | tf_op | source)
XLA Modules:
  0.0 165.3 jit_solution(12188978299267037077)
XLA Ops:
  0.0 160.7 %shard_map.46.y_vmem = bf16[2048,3072]{1,0:T(8,128)(2,1)S(1)} custom-call(bf16[2048,3072]{1,0:T(8,128)(2,1)} %x_hbm.1, bf16[3072,1024]{1,0:T(8,128)(2,1)} %gate_hbm.1, bf16[3072,1024]{1,0:T(8,128)(2,1)} %up_hbm.1, bf16[1024,3072]{1,0:T(8,128)(2,1)} %down_hbm.1), custom_call_target="tpu_custom_call" | custom-call | tf_op jit(solution)/shard_map/pallas_call | solution.py:342
  160.7 4.6 %shard_map.47 = bf16[2048,3072]{1,0:T(8,128)(2,1)} custom-call(bf16[2048,3072]{1,0:T(8,128)(2,1)S(1)} %shard_map.46.y_vmem), custom_call_target="tpu_custom_call" | custom-call | tf_op jit(solution)/shard_map/pallas_call | solution.py:366

commit v7 on v6

--- a/solution.py
+++ b/solution.py
@@ -15,11 +15,12 @@
 STAGE = 4
 OUT_COPIES = 16
 OUT_LIMIT = 1_000_000
-SUM_LAG = ((0, 2, 4, 3), (0, 2, 4, 5))
-DONE_LAG = ((24, 7, 24, 24), (24, 6, 24, 24))
-PARTS = 2
-HEAD = 8
-AHEAD = 4
+SUM_LAG = ((0, 2, 5, 4), (0, 2, 5, 4))
+DONE_LAG = ((24, 6, 24, 24), (24, 6, 24, 24))
+PARTS = 1
+HEAD = 6
+AHEAD = 5
+DOWN_AT = 2
 
 
 def by_place(core, place, rows):
@@ -254,12 +255,10 @@
             gate_copy(k + AHEAD).start()
             up_copy(k + AHEAD).start()
 
-        @pl.when(k + AHEAD >= HEAD)
-        def _():
-            down_copy(k + AHEAD - HEAD).start()
-
-        @pl.when(k == HEAD - 1)
-        def _():
+        @pl.when(k == DOWN_AT)
+        def _():
+            for t in range(tiles):
+                down_copy(t).start()
             fetch_x(1)
 
         xs = x_buf[0, :, depth_slice(k)]

time: 165 us -> 164 us (level)
  no operation moved by 1% of the time
where the time goes in v7:
time: 164 us
  Pallas kernels  164 us (100%)
    pallas_call x1, Pallas kernels, block(): pl.pallas_call(functools.partial(kernel, chunk, tiles), out_shape=pltpu.V...  159 us
    pallas_call x1, Pallas kernels, block(): pl.pallas_call(put_out, out_shape=jax.ShapeDtypeStruct((rows, depth), jnp...  4.57 us

profile of v7, /device:TPU:0, one launch (start us, length us, event | category | flops | bytes accessed | tf_op | source)
XLA Modules:
  0.0 164.1 jit_solution(14614894771676813550)
XLA Ops:
  0.0 159.5 %shard_map.46.y_vmem = bf16[2048,3072]{1,0:T(8,128)(2,1)S(1)} custom-call(bf16[2048,3072]{1,0:T(8,128)(2,1)} %x_hbm.1, bf16[3072,1024]{1,0:T(8,128)(2,1)} %gate_hbm.1, bf16[3072,1024]{1,0:T(8,128)(2,1)} %up_hbm.1, bf16[1024,3072]{1,0:T(8,128)(2,1)} %down_hbm.1), custom_call_target="tpu_custom_call" | custom-call | tf_op jit(solution)/shard_map/pallas_call | solution.py:341
  159.5 4.6 %shard_map.47 = bf16[2048,3072]{1,0:T(8,128)(2,1)} custom-call(bf16[2048,3072]{1,0:T(8,128)(2,1)S(1)} %shard_map.46.y_vmem), custom_call_target="tpu_custom_call" | custom-call | tf_op jit(solution)/shard_map/pallas_call | solution.py:365

commit v8 on v7

--- a/solution.py
+++ b/solution.py
@@ -13,6 +13,12 @@
 TILES = 4
 RING = 16
 STAGE = 4
+OUT_COPIES = 16
+OUT_LIMIT = 1_000_000
+SUM_LAG = ((0, 2, 5, 4), (0, 2, 5, 4))
+DONE_LAG = ((24, 6, 24, 24), (24, 6, 24, 24))
+PARTS = 1
+HEAD = 6
 OUT_COPIES = 16
 OUT_LIMIT = 1_000_000
 SUM_LAG = ((0, 2, 5, 4), (0, 2, 5, 4))
@@ -115,9 +121,16 @@
         hidden[slot, :, unit_slice(t)] = activate(dot(xs, gate_w[:, unit_slice(t)]), dot(xs, up_w[:, unit_slice(t)]))
 
     fetch_x(0)
-    for k in range(AHEAD):
+    @pl.loop(0, HEAD)
+    def _(k):
         gate_copy(k).start()
         up_copy(k).start()
+
+    @pl.loop(0, tiles)
+    def _(t):
+        down_copy(t).start()
+
+    fetch_x(1)
 
     def stage_copy(i):
         slot = lax.rem(i, STAGE)
@@ -249,17 +262,6 @@
     def _(k):
         gate_copy(k).wait()
         up_copy(k).wait()
-
-        @pl.when(k + AHEAD < HEAD)
-        def _():
-            gate_copy(k + AHEAD).start()
-            up_copy(k + AHEAD).start()
-
-        @pl.when(k == DOWN_AT)
-        def _():
-            for t in range(tiles):
-                down_copy(t).start()
-            fetch_x(1)
 
         xs = x_buf[0, :, depth_slice(k)]
         gate = dot(xs, gate_w[depth_slice(k)])

time: 164 us -> 164 us (level)
  no operation moved by 1% of the time
where the time goes in v8:
time: 164 us
  Pallas kernels  164 us (100%)
    pallas_call x1, Pallas kernels, block(): pl.pallas_call(functools.partial(kernel, chunk, tiles), out_shape=pltpu.V...  159 us
    pallas_call x1, Pallas kernels, block(): pl.pallas_call(put_out, out_shape=jax.ShapeDtypeStruct((rows, depth), jnp...  4.57 us

profile of v8, /device:TPU:0, one launch (start us, length us, event | category | flops | bytes accessed | tf_op | source)
XLA Modules:
  0.0 163.9 jit_solution(17267523611308766240)
XLA Ops:
  0.0 159.4 %shard_map.46.y_vmem = bf16[2048,3072]{1,0:T(8,128)(2,1)S(1)} custom-call(bf16[2048,3072]{1,0:T(8,128)(2,1)} %x_hbm.1, bf16[3072,1024]{1,0:T(8,128)(2,1)} %gate_hbm.1, bf16[3072,1024]{1,0:T(8,128)(2,1)} %up_hbm.1, bf16[1024,3072]{1,0:T(8,128)(2,1)} %down_hbm.1), custom_call_target="tpu_custom_call" | custom-call | tf_op jit(solution)/shard_map/pallas_call | solution.py:343
  159.4 4.6 %shard_map.47 = bf16[2048,3072]{1,0:T(8,128)(2,1)} custom-call(bf16[2048,3072]{1,0:T(8,128)(2,1)S(1)} %shard_map.46.y_vmem), custom_call_target="tpu_custom_call" | custom-call | tf_op jit(solution)/shard_map/pallas_call | solution.py:367

commit v9 on v7

--- a/solution.py
+++ b/solution.py
@@ -19,8 +19,8 @@
 DONE_LAG = ((24, 6, 24, 24), (24, 6, 24, 24))
 PARTS = 1
 HEAD = 6
-AHEAD = 5
-DOWN_AT = 2
+AHEAD = 4
+DOWN_AT = 3
 
 
 def by_place(core, place, rows):
@@ -115,7 +115,8 @@
         hidden[slot, :, unit_slice(t)] = activate(dot(xs, gate_w[:, unit_slice(t)]), dot(xs, up_w[:, unit_slice(t)]))
 
     fetch_x(0)
-    for k in range(AHEAD):
+    @pl.loop(0, AHEAD)
+    def _(k):
         gate_copy(k).start()
         up_copy(k).start()
 

time: 164 us -> 163 us (level)
  no operation moved by 1% of the time
where the time goes in v9:
time: 163 us
  Pallas kernels  163 us (100%)
    pallas_call x1, Pallas kernels, block(): pl.pallas_call(functools.partial(kernel, chunk, tiles), out_shape=pltpu.V...  158 us
    pallas_call x1, Pallas kernels, block(): pl.pallas_call(put_out, out_shape=jax.ShapeDtypeStruct((rows, depth), jnp...  4.57 us

profile of v9, /device:TPU:0, one launch (start us, length us, event | category | flops | bytes accessed | tf_op | source)
XLA Modules:
  0.0 162.9 jit_solution(17657470878198253669)
XLA Ops:
  0.0 158.3 %shard_map.46.y_vmem = bf16[2048,3072]{1,0:T(8,128)(2,1)S(1)} custom-call(bf16[2048,3072]{1,0:T(8,128)(2,1)} %x_hbm.1, bf16[3072,1024]{1,0:T(8,128)(2,1)} %gate_hbm.1, bf16[3072,1024]{1,0:T(8,128)(2,1)} %up_hbm.1, bf16[1024,3072]{1,0:T(8,128)(2,1)} %down_hbm.1), custom_call_target="tpu_custom_call" | custom-call | tf_op jit(solution)/shard_map/pallas_call | solution.py:342
  158.3 4.6 %shard_map.47 = bf16[2048,3072]{1,0:T(8,128)(2,1)} custom-call(bf16[2048,3072]{1,0:T(8,128)(2,1)S(1)} %shard_map.46.y_vmem), custom_call_target="tpu_custom_call" | custom-call | tf_op jit(solution)/shard_map/pallas_call | solution.py:366

commit v10 on v9

--- a/solution.py
+++ b/solution.py
@@ -17,7 +17,8 @@
 OUT_LIMIT = 1_000_000
 SUM_LAG = ((0, 2, 5, 4), (0, 2, 5, 4))
 DONE_LAG = ((24, 6, 24, 24), (24, 6, 24, 24))
-PARTS = 1
+LAST = 4
+PARTS = 4
 HEAD = 6
 AHEAD = 4
 DOWN_AT = 3
@@ -83,7 +84,7 @@
         pltpu.make_async_copy(x_hbm.at[pl.ds(0, 2 * chunk), :], x_buf.at[slot], x_sem.at[slot]).wait()
 
     depth_tile = depth // HEAD
-    part_tile = col_tile // PARTS
+    part_rows = chunk // PARTS
 
     def unit_slice(t):
         return pl.ds(pl.multiple_of(t * unit_tile, unit_tile), unit_tile)
@@ -139,94 +140,97 @@
         stage_copy(i).start()
         own[lax.rem(i, RING)] = term[:chunk]
 
-    def low_copy(p):
-        return pltpu.make_async_remote_copy(
-            src_ref=sums.at[p], dst_ref=low.at[p], send_sem=sum_sem, recv_sem=low_sem.at[p],
-            device_id=after, device_id_type=MESH,
-        )
-
-    def high_copy(p):
-        return pltpu.make_async_remote_copy(
-            src_ref=sums.at[p], dst_ref=high.at[p], send_sem=sum_sem, recv_sem=high_sem.at[p],
-            device_id=before, device_id_type=MESH,
-        )
-
-    def spread_copy(p):
-        return pltpu.make_async_remote_copy(
-            src_ref=sums.at[p], dst_ref=high.at[p], send_sem=spread_sem, recv_sem=high_sem.at[p],
-            device_id=after, device_id_type=MESH,
-        )
-
-    def pass_copy(p):
-        return pltpu.make_async_remote_copy(
-            src_ref=high.at[p], dst_ref=high.at[p], send_sem=pass_sem, recv_sem=high_sem.at[p],
-            device_id=before, device_id_type=MESH,
-        )
-
-    def deliver(src, m):
-        p = m // PARTS
-        c, column = p // tiles, lax.rem(p, tiles) * col_tile + lax.rem(m, PARTS) * part_tile
+    def message(buffer, p, part):
+        return buffer.at[p] if part is None else buffer.at[p, pl.ds(part * part_rows, part_rows)]
+
+    def arrival(sems, p, part):
+        return sems.at[pieces + (p - (pieces - LAST)) * (PARTS - 1) + part - 1 if part else p]
+
+    def await_message(buffer, sems, p, part):
+        ref = message(buffer, p, part)
+        pltpu.make_async_copy(ref, ref, arrival(sems, p, part)).wait()
+
+    def send(source, target, send_sem, sems, to, p, part):
+        pltpu.make_async_remote_copy(
+            src_ref=message(source, p, part), dst_ref=message(target, p, part), send_sem=send_sem,
+            recv_sem=arrival(sems, p, part), device_id=to, device_id_type=MESH,
+        ).start()
+
+    def deliver(buffer, p, part):
+        c, t = p // tiles, lax.rem(p, tiles)
+        count = chunk if part is None else part_rows
+        row = core * half + c * chunk + (part or 0) * part_rows
+        src = message(buffer, p, part)
         block = y_hbm.at[
-            pl.ds(pl.multiple_of(core * half + c * chunk, chunk), chunk),
-            pl.ds(pl.multiple_of(column, part_tile), part_tile),
+            pl.ds(pl.multiple_of(row, count), count), pl.ds(pl.multiple_of(t * col_tile, col_tile), col_tile)
         ]
         pltpu.make_async_remote_copy(
             src_ref=src, dst_ref=block, send_sem=give_sem, recv_sem=take_sem, device_id=other, device_id_type=MESH,
         ).start()
         pltpu.make_async_copy(src, block, y_sem).start()
 
+    def combine_message(p, part):
+        rows = slice(None) if part is None else slice(part * part_rows, (part + 1) * part_rows)
+
+        def here():
+            return own[lax.rem(p, RING), rows] + theirs[p, rows].astype(jnp.float32)
+
+        @pl.when(jnp.logical_not(inner))
+        def _():
+            sums[p, rows] = here().astype(jnp.bfloat16)
+
+        @pl.when(inner)
+        def _():
+            await_message(low, low_sem, p, part)
+
+        @pl.when(place == 1)
+        def _():
+            sums[p, rows] = (here() + low[p, rows].astype(jnp.float32)).astype(jnp.bfloat16)
+
+        @pl.when(place == 2)
+        def _():
+            await_message(high, high_sem, p, part)
+            total = here() + low[p, rows].astype(jnp.float32) + high[p, rows].astype(jnp.float32)
+            sums[p, rows] = total.astype(jnp.bfloat16)
+
+        @pl.when(place < 2)
+        def _():
+            send(sums, low, sum_sem, low_sem, after, p, part)
+
+        @pl.when(place >= 2)
+        def _():
+            send(sums, high, sum_sem, high_sem, before, p, part)
+
+        @pl.when(place == 2)
+        def _():
+            send(sums, high, spread_sem, high_sem, after, p, part)
+            deliver(sums, p, part)
+
+    def finish_message(p, part):
+        await_message(high, high_sem, p, part)
+
+        @pl.when(place == 1)
+        def _():
+            send(high, high, pass_sem, high_sem, before, p, part)
+
+        deliver(high, p, part)
+
+    def by_message(p, action):
+        @pl.when(p < pieces - LAST)
+        def _():
+            action(p, None)
+
+        @pl.when(p >= pieces - LAST)
+        def _():
+            for part in range(PARTS):
+                action(p, part)
+
     def combine(p):
         pltpu.make_async_copy(theirs.at[p], theirs.at[p], theirs_sem.at[p]).wait()
-        for part in range(PARTS):
-            combine_part(p, part)
-
-    def combine_part(p, part):
-        m = p * PARTS + part
-        columns = slice(part * part_tile, (part + 1) * part_tile)
-
-        def here():
-            return own[lax.rem(p, RING), :, columns] + theirs[p, :, columns].astype(jnp.float32)
-
-        @pl.when(jnp.logical_not(inner))
-        def _():
-            sums[m] = here().astype(jnp.bfloat16)
-
-        @pl.when(inner)
-        def _():
-            pltpu.make_async_copy(low.at[m], low.at[m], low_sem.at[m]).wait()
-
-        @pl.when(place == 1)
-        def _():
-            sums[m] = (here() + low[m].astype(jnp.float32)).astype(jnp.bfloat16)
-
-        @pl.when(place == 2)
-        def _():
-            pltpu.make_async_copy(high.at[m], high.at[m], high_sem.at[m]).wait()
-            sums[m] = (here() + low[m].astype(jnp.float32) + high[m].astype(jnp.float32)).astype(jnp.bfloat16)
-
-        @pl.when(place < 2)
-        def _():
-            low_copy(m).start()
-
-        @pl.when(place >= 2)
-        def _():
-            high_copy(m).start()
-
-        @pl.when(place == 2)
-        def _():
-            spread_copy(m).start()
-            deliver(sums.at[m], m)
+        by_message(p, combine_message)
 
     def finish(p):
-        for part in range(PARTS):
-            m = p * PARTS + part
-            pltpu.make_async_copy(high.at[m], high.at[m], high_sem.at[m]).wait()
-
-            @pl.when(place == 1)
-            def _():
-                pass_copy(m).start()
-
-            deliver(high.at[m], m)
+        by_message(p, finish_message)
 
     sum_lag = by_place(core, place, SUM_LAG)
     done_lag = by_place(core, place, DONE_LAG)
@@ -326,7 +330,7 @@
     rows = y_vmem.shape[0] // OUT_COPIES
     for k in range(OUT_COPIES):
         part = pl.ds(k * rows, rows)
-        pltpu.make_async_copy(y_vmem.at[part], y_hbm.at[part], sem).start()
+        pltpu.make_async_copy(y_vmem.at[part], y_hbm.at[part], sem).start(priority=k % 2)
     pltpu.make_async_copy(y_vmem, y_hbm, sem).wait()
 
 
@@ -335,8 +339,8 @@
     units = w_gate.shape[1]
     pieces = rows // 2 // chunk * tiles
     piece = (chunk, depth // tiles)
-    messages = pieces * PARTS
-    buffers = pltpu.VMEM((messages, chunk, depth // tiles // PARTS), jnp.bfloat16)
+    messages = pieces + LAST * (PARTS - 1)
+    buffers = pltpu.VMEM((pieces,) + piece, jnp.bfloat16)
     dma = pltpu.SemaphoreType.DMA
     anywhere = pl.BlockSpec(memory_space=pl.ANY)
     y = pl.pallas_call(
@@ -354,7 +358,7 @@
             pltpu.VMEM((2 * chunk, units), jnp.float32),
             pltpu.VMEM((RING,) + piece, jnp.float32),
             pltpu.VMEM((STAGE,) + piece, jnp.bfloat16),
-            pltpu.VMEM((pieces,) + piece, jnp.bfloat16), buffers, buffers, buffers,
+            buffers, buffers, buffers, buffers,
             dma((2,)), dma((HEAD,)), dma((HEAD,)), dma((tiles,)), dma((STAGE,)),
             dma((pieces,)), dma((messages,)), dma((messages,)),
             dma, dma, dma, dma, dma, dma,

time: 163 us -> 163 us (level)
  no operation moved by 1% of the time
where the time goes in v10:
time: 163 us
  Pallas kernels  163 us (100%)
    pallas_call x1, Pallas kernels, block(): pl.pallas_call(functools.partial(kernel, chunk, tiles), out_shape=pltpu.V...  158 us
    pallas_call x1, Pallas kernels, block(): pl.pallas_call(put_out, out_shape=jax.ShapeDtypeStruct((rows, depth), jnp...  4.57 us

profile of v10, /device:TPU:0, one launch (start us, length us, event | category | flops | bytes accessed | tf_op | source)
XLA Modules:
  0.0 162.9 jit_solution(13147926337394810872)
XLA Ops:
  0.0 158.4 %shard_map.46.y_vmem = bf16[2048,3072]{1,0:T(8,128)(2,1)S(1)} custom-call(bf16[2048,3072]{1,0:T(8,128)(2,1)} %x_hbm.1, bf16[3072,1024]{1,0:T(8,128)(2,1)} %gate_hbm.1, bf16[3072,1024]{1,0:T(8,128)(2,1)} %up_hbm.1, bf16[1024,3072]{1,0:T(8,128)(2,1)} %down_hbm.1), custom_call_target="tpu_custom_call" | custom-call | tf_op jit(solution)/shard_map/pallas_call | solution.py:346
  158.4 4.6 %shard_map.47 = bf16[2048,3072]{1,0:T(8,128)(2,1)} custom-call(bf16[2048,3072]{1,0:T(8,128)(2,1)S(1)} %shard_map.46.y_vmem), custom_call_target="tpu_custom_call" | custom-call | tf_op jit(solution)/shard_map/pallas_call | solution.py:370

commit v11 on v9

--- a/solution.py
+++ b/solution.py
@@ -15,7 +15,7 @@
 STAGE = 4
 OUT_COPIES = 16
 OUT_LIMIT = 1_000_000
-SUM_LAG = ((0, 2, 5, 4), (0, 2, 5, 4))
+SUM_LAG = ((0, 2, 5, 3), (0, 2, 5, 3))
 DONE_LAG = ((24, 6, 24, 24), (24, 6, 24, 24))
 PARTS = 1
 HEAD = 6
@@ -279,29 +279,34 @@
     hidden[0] = activate(first_gate[...], first_up[...])
     pl.semaphore_wait(barrier, jnp.where(inner, 3, 2))
 
+    def terms_of(i):
+        @pl.when(i < tiles)
+        def _():
+            down_copy(i).wait()
+
+        terms(i // tiles, lax.rem(i, tiles))
+
+    terms_of(jnp.int32(0))
+
     @pl.loop(0, pieces + LONGEST)
     def _(i):
         c, t = i // tiles, lax.rem(i, tiles)
 
-        @pl.when(i < pieces)
-        def _():
-            @pl.when(c == 0)
-            def _():
-                down_copy(t).wait()
-
-            @pl.when(jnp.logical_and(t == 0, c + 2 < chunks))
-            def _():
-                fetch_x(c + 2)
-
-            @pl.when(jnp.logical_and(t == 0, c + 1 < chunks))
-            def _():
-                wait_x(c + 1)
-
-            terms(c, t)
-
-            @pl.when(c + 1 < chunks)
-            def _():
-                project(c + 1, t)
+        @pl.when(jnp.logical_and(t == 0, c + 2 < chunks))
+        def _():
+            fetch_x(c + 2)
+
+        @pl.when(jnp.logical_and(t == 0, c + 1 < chunks))
+        def _():
+            wait_x(c + 1)
+
+        @pl.when(c + 1 < chunks)
+        def _():
+            project(c + 1, t)
+
+        @pl.when(i + 1 < pieces)
+        def _():
+            terms_of(i + 1)
 
         trail(i)
 

time: 163 us -> 163 us (level)
  no operation moved by 1% of the time
where the time goes in v11:
time: 163 us
  Pallas kernels  163 us (100%)
    pallas_call x1, Pallas kernels, block(): pl.pallas_call(functools.partial(kernel, chunk, tiles), out_shape=pltpu.V...  159 us
    pallas_call x1, Pallas kernels, block(): pl.pallas_call(put_out, out_shape=jax.ShapeDtypeStruct((rows, depth), jnp...  4.57 us

profile of v11, /device:TPU:0, one launch (start us, length us, event | category | flops | bytes accessed | tf_op | source)
XLA Modules:
  0.0 163.4 jit_solution(3358646350945015523)
XLA Ops:
  0.0 158.8 %shard_map.46.y_vmem = bf16[2048,3072]{1,0:T(8,128)(2,1)S(1)} custom-call(bf16[2048,3072]{1,0:T(8,128)(2,1)} %x_hbm.1, bf16[3072,1024]{1,0:T(8,128)(2,1)} %gate_hbm.1, bf16[3072,1024]{1,0:T(8,128)(2,1)} %up_hbm.1, bf16[1024,3072]{1,0:T(8,128)(2,1)} %down_hbm.1), custom_call_target="tpu_custom_call" | custom-call | tf_op jit(solution)/shard_map/pallas_call | solution.py:347
  158.8 4.6 %shard_map.47 = bf16[2048,3072]{1,0:T(8,128)(2,1)} custom-call(bf16[2048,3072]{1,0:T(8,128)(2,1)S(1)} %shard_map.46.y_vmem), custom_call_target="tpu_custom_call" | custom-call | tf_op jit(solution)/shard_map/pallas_call | solution.py:371

commit v12 on v9

--- a/solution.py
+++ b/solution.py
@@ -15,7 +15,7 @@
 STAGE = 4
 OUT_COPIES = 16
 OUT_LIMIT = 1_000_000
-SUM_LAG = ((0, 2, 5, 4), (0, 2, 5, 4))
+SUM_LAG = ((0, 2, 5, 3), (0, 2, 5, 5))
 DONE_LAG = ((24, 6, 24, 24), (24, 6, 24, 24))
 PARTS = 1
 HEAD = 6

time: 163 us -> 164 us (level)
  no operation moved by 1% of the time
where the time goes in v12:
time: 164 us
  Pallas kernels  164 us (100%)
    pallas_call x1, Pallas kernels, block(): pl.pallas_call(functools.partial(kernel, chunk, tiles), out_shape=pltpu.V...  159 us
    pallas_call x1, Pallas kernels, block(): pl.pallas_call(put_out, out_shape=jax.ShapeDtypeStruct((rows, depth), jnp...  4.57 us

profile of v12, /device:TPU:0, one launch (start us, length us, event | category | flops | bytes accessed | tf_op | source)
XLA Modules:
  0.0 163.7 jit_solution(5303406786266289256)
XLA Ops:
  0.0 159.2 %shard_map.46.y_vmem = bf16[2048,3072]{1,0:T(8,128)(2,1)S(1)} custom-call(bf16[2048,3072]{1,0:T(8,128)(2,1)} %x_hbm.1, bf16[3072,1024]{1,0:T(8,128)(2,1)} %gate_hbm.1, bf16[3072,1024]{1,0:T(8,128)(2,1)} %up_hbm.1, bf16[1024,3072]{1,0:T(8,128)(2,1)} %down_hbm.1), custom_call_target="tpu_custom_call" | custom-call | tf_op jit(solution)/shard_map/pallas_call | solution.py:342
  159.2 4.6 %shard_map.47 = bf16[2048,3072]{1,0:T(8,128)(2,1)} custom-call(bf16[2048,3072]{1,0:T(8,128)(2,1)S(1)} %shard_map.46.y_vmem), custom_call_target="tpu_custom_call" | custom-call | tf_op jit(solution)/shard_map/pallas_call | solution.py:366

commit v13 on v12

--- a/solution.py
+++ b/solution.py
@@ -15,7 +15,7 @@
 STAGE = 4
 OUT_COPIES = 16
 OUT_LIMIT = 1_000_000
-SUM_LAG = ((0, 2, 5, 3), (0, 2, 5, 5))
+SUM_LAG = ((0, 2, 5, 4), (0, 2, 5, 3))
 DONE_LAG = ((24, 6, 24, 24), (24, 6, 24, 24))
 PARTS = 1
 HEAD = 6

time: 164 us -> 163 us (level)
  no operation moved by 1% of the time
where the time goes in v13:
time: 163 us
  Pallas kernels  163 us (100%)
    pallas_call x1, Pallas kernels, block(): pl.pallas_call(functools.partial(kernel, chunk, tiles), out_shape=pltpu.V...  158 us
    pallas_call x1, Pallas kernels, block(): pl.pallas_call(put_out, out_shape=jax.ShapeDtypeStruct((rows, depth), jnp...  4.57 us

profile of v13, /device:TPU:0, one launch (start us, length us, event | category | flops | bytes accessed | tf_op | source)
XLA Modules:
  0.0 162.9 jit_solution(6133262808090604427)
XLA Ops:
  0.0 158.3 %shard_map.46.y_vmem = bf16[2048,3072]{1,0:T(8,128)(2,1)S(1)} custom-call(bf16[2048,3072]{1,0:T(8,128)(2,1)} %x_hbm.1, bf16[3072,1024]{1,0:T(8,128)(2,1)} %gate_hbm.1, bf16[3072,1024]{1,0:T(8,128)(2,1)} %up_hbm.1, bf16[1024,3072]{1,0:T(8,128)(2,1)} %down_hbm.1), custom_call_target="tpu_custom_call" | custom-call | tf_op jit(solution)/shard_map/pallas_call | solution.py:342
  158.3 4.6 %shard_map.47 = bf16[2048,3072]{1,0:T(8,128)(2,1)} custom-call(bf16[2048,3072]{1,0:T(8,128)(2,1)S(1)} %shard_map.46.y_vmem), custom_call_target="tpu_custom_call" | custom-call | tf_op jit(solution)/shard_map/pallas_call | solution.py:366
